TPU v7x, 32 devices: a whole 2x2x4 slice. The times are simulated.
32 devices in a mesh: head: 2 (over core), blk: 4 (over z), rep: 4 (over y, x).
Axes of the slice: x: 2, y: 2, z: 4, core: 2. Of those that a mesh axis runs over, the one named last changes fastest.
Arguments:
- queries: bfloat16 [2048, 768], P(('blk', 'rep'), 'head'), may hold values from -400 to 400
- keys: bfloat16 [2048, 256], P(('blk', 'rep'), 'head'), may hold values from -6 to 6
- values: bfloat16 [2048, 256], P(('blk', 'rep'), 'head'), may hold values from -18 to 18
- stretch_order: int32 [16], replicated, may hold values from 0 to 15, each once
- out_weight: bfloat16 [768, 3072], P('head'), may hold values from -0.21875 to 0.21875
Outputs:
- mixed_rows: bfloat16 [2048, 3072], P(('blk', 'rep'), 'head')
- log_sum_exp: float32 [6, 2048], P('head', ('blk', 'rep'))
Inputs may be any that keep to these rules, and one draw needn't show every extreme that they name: `stretch_order`: each stretch number appears once.
All inputs are finite; a program needn't handle non-finite values.
Results may differ from a plain program's by a relative error of at most 0.02.
Values may be sent and summed in bfloat16 or wider, within the bound.
A program may use at most 128 MiB of HBM per device.

v0:
```python
import functools
import math

import jax
import jax.numpy as jnp
from jax import lax
from jax.experimental import pallas as pl
from jax.experimental.pallas import tpu as pltpu
from jax.sharding import PartitionSpec as P

DH = 128
NEG_FILL = -1e30
MESH = pl.DeviceIdType.MESH
UNROLL_LIMIT = 8
FAR_FIRST = False
SWAP = True
FAR_DIAG = False
FAR_X = ()
FAR_Y = ()
VMEM_LIMIT = 24 * 1024 * 1024
DIRECT_DIAG = 3


def project(att, weight, tok):
    out = None
    for g in range(att.shape[1] // tok):
        term = lax.dot_general(
            att[:, g * tok:(g + 1) * tok], weight[g * DH:(g + 1) * DH, :],
            (((0,), (0,)), ((), ())), preferred_element_type=jnp.float32,
        )
        out = term if out is None else out + term
    return out


def finish_kernel(own_ref, att, w_buf, sums_ref, mixed_ref, lse_ref):
    lse_ref[...] = sums_ref[...]
    other = project(att[1], w_buf[1], own_ref.shape[0])
    mixed_ref[...] = (own_ref[...] + other).astype(mixed_ref.dtype)


def kernel(
    spans, q_ref, k_ref, v_ref, order_hbm, w_ref, own_ref, att, w_buf, lse_ref,
    order_ref, q_buf, kv, qt, acc, top, total,
    local_sem, f_send, z_send, z_recv, x_send, x_recv, y_send, y_recv, d_send, d_recv,
    w_send, w_recv, a_send, a_recv,
):
    tok, width = q_ref.shape
    group = width // DH
    rows = group * tok
    half = own_ref.shape[1]
    head = lax.axis_index("head")
    b = lax.axis_index("blk")
    r = lax.axis_index("rep")
    other = 1 - head
    rep_x = r + 1 - 2 * (r % 2)
    rep_y = (r + 2) % 4
    rep_d = 3 - r

    def peer(s):
        upper = b // (spans // 2)
        folded = b + upper * (spans - 1 - 2 * b)
        place = s - (folded + spans - s) // spans
        if SWAP and spans == 4 and s >= 2:
            place = place + (5 - 2 * s) * (1 - (folded + spans - 1) // spans)
        return place + upper * (spans - 1 - 2 * place)

    def for_each(count, step, start=0):
        if count - start <= UNROLL_LIMIT:
            for s in range(start, count):
                step(s)
        else:
            def run(s, carry):
                step(s)
                return carry
            lax.fori_loop(start, count, run, 0)

    loads = [
        pltpu.make_async_copy(k_ref, kv.at[0, b, 0], local_sem.at[0]),
        pltpu.make_async_copy(v_ref, kv.at[0, b, 1], local_sem.at[1]),
        pltpu.make_async_copy(q_ref, q_buf, local_sem.at[2]),
        pltpu.make_async_copy(order_hbm, order_ref, local_sem.at[4]),
    ]
    for load in loads:
        load.start()
    barrier = pltpu.get_barrier_semaphore()

    pl.semaphore_signal(barrier, inc=1, device_id={"rep": rep_x}, device_id_type=MESH)
    pl.semaphore_signal(barrier, inc=1, device_id={"rep": rep_y}, device_id_type=MESH)
    pl.semaphore_signal(barrier, inc=1, device_id={"head": other}, device_id_type=MESH)
    if DIRECT_DIAG <= spans:
        pl.semaphore_signal(barrier, inc=1, device_id={"rep": rep_d}, device_id_type=MESH)
    at_end = (b == 0) | (b == spans - 1)
    far = spans - 1 - b

    @pl.when(b > 0)
    def _():
        pl.semaphore_signal(barrier, inc=1, device_id={"blk": b - 1}, device_id_type=MESH)

    @pl.when(b < spans - 1)
    def _():
        pl.semaphore_signal(barrier, inc=1, device_id={"blk": b + 1}, device_id_type=MESH)

    far_reps = [r] + [rep_d] * FAR_DIAG + [rep_x] * bool(FAR_X) + [rep_y] * bool(FAR_Y)

    @pl.when(at_end)
    def _():
        for place in far_reps:
            pl.semaphore_signal(barrier, inc=1, device_id={"blk": far, "rep": place}, device_id_type=MESH)

    inner = 2 - (spans - b) // spans - (b + 1) // spans
    line = inner + (2 - inner) * len(far_reps)

    loads[0].wait()
    loads[1].wait()
    pl.semaphore_wait(barrier, line + 3 + (DIRECT_DIAG <= spans))

    def remote(src, dst, send, recv, axis, place):
        return pltpu.make_async_remote_copy(
            src_ref=src, dst_ref=dst, send_sem=send, recv_sem=recv,
            device_id={axis: place}, device_id_type=MESH,
        )

    def z_arrival(p, c):
        return remote(kv.at[0, p, c], kv.at[0, p, c], z_send.at[0, c], z_recv.at[p, c], "blk", p)

    def is_far(p):
        return (p - b == spans - 1) | (b - p == spans - 1)

    def far_copy(j, c):
        recv = [z_recv, x_recv, y_recv, d_recv][j]
        return pltpu.make_async_remote_copy(
            src_ref=kv.at[0, b, c], dst_ref=kv.at[j, b, c],
            send_sem=f_send.at[j, c], recv_sem=recv.at[b, c],
            device_id={"blk": far, "rep": [r, rep_x, rep_y, rep_d][j]}, device_id_type=MESH,
        )

    def all_far(act, js=(0, 1, 2, 3)):
        @pl.when(at_end)
        def _():
            for j in js:
                for c in [(0, 1), FAR_X, FAR_Y, (0, 1) if FAR_DIAG else ()][j]:
                    act(far_copy(j, c))

    def unless_far(p, c, skipped, act, copy):
        if c in skipped:
            @pl.when(jnp.logical_not(is_far(p)))
            def _():
                act(copy)
        else:
            act(copy)

    def x_copy(p, c):
        return remote(kv.at[0, p, c], kv.at[1, p, c], x_send.at[p, c], x_recv.at[p, c], "rep", rep_x)

    def y_copy(p, c):
        return remote(kv.at[0, p, c], kv.at[2, p, c], y_send.at[p, c], y_recv.at[p, c], "rep", rep_y)

    def d_copy(p, c):
        return remote(
            kv.at[1 + c, p, c], kv.at[3, p, c], d_send.at[p, c], d_recv.at[p, c],
            "rep", rep_x if c else rep_y,
        )

    def d_direct(p, c):
        return remote(kv.at[0, p, c], kv.at[3, p, c], d_send.at[p, c], d_recv.at[p, c], "rep", rep_d)

    def start(copy):
        copy.start()

    def each_plane(p, act, kinds=(0, 1)):
        for c in kinds:
            unless_far(p, c, FAR_X, act, x_copy(p, c))
            unless_far(p, c, FAR_Y, act, y_copy(p, c))

    def hop(p, c, down):
        return remote(kv.at[0, p, c], kv.at[0, p, c], z_send.at[p, c + 2 * down], z_recv.at[p, c], "blk", b + 1 - 2 * down)

    def pass_on(p, act, kinds=(0, 1)):
        @pl.when((p >= b) & (b > 0) & (p - b < spans - 2))
        def _():
            for c in kinds:
                act(hop(p, c, 1))

        @pl.when((p <= b) & (b < spans - 1) & (b - p < spans - 2))
        def _():
            for c in kinds:
                act(hop(p, c, 0))

    if FAR_FIRST:
        all_far(start, (0,))
    pass_on(b, start)
    each_plane(b, start)
    if not FAR_FIRST:
        all_far(start, (0,))
    all_far(start, (3, 1, 2))

    w_local = pltpu.make_async_copy(
        w_ref.at[:, pl.ds(pl.multiple_of(head * half, DH), half)], w_buf.at[0], local_sem.at[3]
    )
    w_remote = remote(
        w_ref.at[:, pl.ds(pl.multiple_of(other * half, DH), half)], w_buf.at[1],
        w_send, w_recv, "head", other,
    )
    w_local.start()
    w_remote.start()

    loads[2].wait()
    loads[3].wait()
    for g in range(group):
        qt[:, g * tok:(g + 1) * tok] = (
            q_buf[:, g * DH:(g + 1) * DH].astype(jnp.float32).T.astype(jnp.bfloat16)
        )
    key_at = lax.broadcasted_iota(jnp.int32, (tok, rows), 0)
    query_at = lax.broadcasted_iota(jnp.int32, (tok, rows), 1) % tok
    lead = key_at - query_at
    mine = order_ref[b * 4 + r]
    factor = DH ** (-0.5) * math.log2(math.e)

    def attend(j, p, first=False):
        rep = [r, rep_x, rep_y, rep_d][j]
        scores = jnp.dot(kv[j, p, 0], qt[...], preferred_element_type=jnp.float32) * factor
        gap = (mine - order_ref[p * 4 + rep]) * tok
        scores = jnp.where(lead <= gap, scores, NEG_FILL)
        best = jnp.max(scores, axis=0, keepdims=True)
        if not first:
            before = top[...]
            best = jnp.maximum(best, before)
        weights = jnp.exp2(scores - best)
        part = jnp.sum(weights, axis=0, keepdims=True)
        numer = lax.dot_general(
            kv[j, p, 1], weights.astype(jnp.bfloat16), (((0,), (0,)), ((), ())),
            preferred_element_type=jnp.float32,
        )
        if first:
            total[...] = part
            acc[...] = numer
        else:
            shrink = jnp.exp2(before - best)
            total[...] = total[...] * shrink + part
            acc[...] = acc[...] * shrink + numer
        top[...] = best

    def from_line(s):
        p = peer(s)
        for c in (0, 1):
            z_arrival(p, c).wait_recv()
            pass_on(p, start, (c,))
            each_plane(p, start, (c,))
        if spans <= UNROLL_LIMIT and s >= DIRECT_DIAG:
            for c in (0, 1):
                unless_far(p, c, (0, 1) if FAR_DIAG else (), start, d_direct(p, c))

    def to_diagonal(p, direct=False):
        skipped = (0, 1) if FAR_DIAG else ()
        x_copy(p, 0).wait_recv()
        if not direct:
            unless_far(p, 0, skipped, start, d_copy(p, 0))
        y_copy(p, 1).wait_recv()
        if not direct:
            unless_far(p, 1, skipped, start, d_copy(p, 1))
        x_copy(p, 1).wait_recv()
        y_copy(p, 0).wait_recv()

    def from_diagonal(p):
        d_copy(p, 0).wait_recv()
        d_copy(p, 1).wait_recv()

    attend(0, b, True)
    if spans <= UNROLL_LIMIT:
        places = [b] + [peer(s) for s in range(1, spans)]
        for s in range(1, spans + 2):
            if s < spans:
                from_line(s)
            if s <= spans:
                to_diagonal(places[s - 1], s - 1 >= DIRECT_DIAG)
            if s < spans:
                attend(0, places[s])
            if s <= spans:
                attend(1, places[s - 1])
                attend(2, places[s - 1])
            if s >= 2:
                from_diagonal(places[s - 2])
                attend(3, places[s - 2])
    else:
        for_each(spans, from_line, 1)
        for_each(spans, to_diagonal)
        for_each(spans, from_diagonal)

        def near(s):
            attend(0, peer(s))

        def others(p):
            for j in (1, 2, 3):
                attend(j, p)

        for_each(spans, near, 1)
        for_each(spans, others)

    att[0] = (acc[...] / total[...]).astype(jnp.bfloat16)
    swap = remote(att.at[0], att.at[1], a_send, a_recv, "head", other)
    swap.start()
    sums = (top[...] + jnp.log2(total[...])) * math.log(2.0)
    for g in range(group):
        lse_ref[g:g + 1, :] = sums[:, g * tok:(g + 1) * tok]

    w_local.wait()
    own_ref[...] = project(att[0], w_buf[0], tok)
    w_remote.wait_recv()
    swap.wait_recv()

    def sent(copy):
        copy.wait_send()

    def finish(p):
        pass_on(p, sent)
        each_plane(p, sent)
        for c in (0, 1):
            unless_far(p, c, (0, 1) if FAR_DIAG else (), sent, d_copy(p, c))

    for_each(spans, finish)
    all_far(sent)
    w_remote.wait_send()
    swap.wait_send()


def solution(mesh):
    spans = mesh.shape["blk"]

    def body(queries, keys, values, stretch_order, out_weight):
        tok, width = queries.shape
        group = width // DH
        rows = group * tok
        half = out_weight.shape[1] // mesh.shape["head"]
        anywhere = pl.BlockSpec(memory_space=pltpu.HBM)
        vmem = pl.BlockSpec(memory_space=pltpu.VMEM)
        dma = pltpu.SemaphoreType.DMA
        gathered = pl.pallas_call(
            functools.partial(kernel, spans),
            out_shape=(
                pltpu.VMEM((tok, half), jnp.float32),
                pltpu.VMEM((2, DH, rows), jnp.bfloat16),
                pltpu.VMEM((2, width, half), jnp.bfloat16),
                pltpu.VMEM((group, tok), jnp.float32),
            ),
            in_specs=[anywhere] * 5,
            out_specs=(vmem,) * 4,
            scratch_shapes=[
                pltpu.SMEM(stretch_order.shape, jnp.int32),
                pltpu.VMEM((tok, width), jnp.bfloat16),
                pltpu.VMEM((4, spans, 2, tok, DH), jnp.bfloat16),
                pltpu.VMEM((DH, rows), jnp.bfloat16),
                pltpu.VMEM((DH, rows), jnp.float32),
                pltpu.VMEM((1, rows), jnp.float32),
                pltpu.VMEM((1, rows), jnp.float32),
                dma((5,)), dma((4, 2)),
                dma((spans, 4)), dma((spans, 2)),
                dma((spans, 2)), dma((spans, 2)),
                dma((spans, 2)), dma((spans, 2)),
                dma((spans, 2)), dma((spans, 2)),
                dma, dma, dma, dma,
            ],
            compiler_params=pltpu.CompilerParams(collective_id=0, has_side_effects=True, vmem_limit_bytes=VMEM_LIMIT),
        )(*(
            pltpu.with_memory_space_constraint(array, pltpu.HBM)
            for array in (queries, keys, values, stretch_order, out_weight)
        ))
        return pl.pallas_call(
            finish_kernel,
            out_shape=(
                jax.ShapeDtypeStruct((tok, half), jnp.bfloat16),
                jax.ShapeDtypeStruct((group, tok), jnp.float32),
            ),
            in_specs=[vmem] * 4,
            out_specs=(vmem, vmem),
            compiler_params=pltpu.CompilerParams(vmem_limit_bytes=VMEM_LIMIT),
        )(*gathered)

    in_specs = (
        P(("blk", "rep"), "head"),
        P(("blk", "rep"), "head"),
        P(("blk", "rep"), "head"),
        P(),
        P("head", None),
    )
    out_specs = (P(("blk", "rep"), "head"), P("head", ("blk", "rep")))
    return jax.shard_map(body, mesh=mesh, in_specs=in_specs, out_specs=out_specs, check_vma=False)
```

profile of v0, /device:TPU:0, one launch (start us, length us, event | category | flops | bytes accessed | tf_op | source)
XLA Modules:
  0.0 21.8 jit_solution(10153881938229851411)
XLA Ops:
  0.6 19.9 %shard_map.68 = (f32[128,1536]{1,0:T(8,128)S(1)}, bf16[2,128,384]{2,1,0:T(8,128)(2,1)S(1)}, bf16[2,384,1536]{2,1,0:T(8,128)(2,1)S(1)}, f32[3,128]{1,0:T(4,128)S(1)}) custom-call(bf16[128,384]{1,0:T(8,128)(2,1)} %q_ref.1, bf16[128,128]{1,0:T(8,128)(2,1)} %k_ref.1, bf16[128,128]{1,0:T(8,128)(2,1)} %v_ref.1, s32[16]{0:T(128)} %order_hbm.1, bf16[384,3072]{1,0:T(8,128)(2,1)} %w_ref.1), custom_call_target="tpu_custom_call" | custom-call | tf_op jit(solution)/shard_map/pallas_call | solution.py:337
  20.6 1.2 %shard_map.69 = (bf16[128,1536]{1,0:T(8,128)(2,1)}, f32[3,128]{1,0:T(4,128)}) custom-call(f32[128,1536]{1,0:T(8,128)S(1)} %get-tuple-element.6.own_ref, bf16[2,128,384]{2,1,0:T(8,128)(2,1)S(1)} %get-tuple-element.7.att, bf16[2,384,1536]{2,1,0:T(8,128)(2,1)S(1)} %get-tuple-element.8.w_buf, f32[3,128]{1,0:T(4,128)S(1)} %get-tuple-element.9.sums_ref), custom_call_target="tpu_custom_call" | custom-call | tf_op jit(solution)/shard_map/pallas_call | solution.py:367
where the time goes:
time: 22 us; the launch traced here: 21.8 us
  Pallas kernels  21.2 us (96%)
  between operations  0.64 us (3%)
    pallas_call x1, Pallas kernels, body(): pl.pallas_call(functools.partial(kernel, spans), out_shape=(pltpu.VMEM((t...  19.9 us
    pallas_call x1, Pallas kernels, body(): pl.pallas_call(finish_kernel, out_shape=(jax.ShapeDtypeStruct((tok, half)...  1.24 us

commit v1 on v0

--- a/solution.py
+++ b/solution.py
@@ -19,6 +19,43 @@
 FAR_Y = ()
 VMEM_LIMIT = 24 * 1024 * 1024
 DIRECT_DIAG = 3
+
+TREES = (
+    (
+        (
+            (-1, 0, 0, 0, 0, 1, 4, 4, 4, 8, 8, 7, 0, 12, 12, 7),
+            (4, 0, 6, 7, -1, 4, 4, 4, 4, 8, 8, 7, 8, 12, 12, 7),
+            (8, 0, 0, 11, 0, 1, 2, 11, -1, 8, 8, 8, 8, 12, 12, 11),
+            (12, 0, 0, 15, 12, 4, 4, 4, 12, 13, 8, 15, -1, 12, 12, 12),
+        ),
+        (
+            (-1, 0, 0, 0, 0, 4, 4, 3, 0, 8, 8, 8, 0, 12, 12, 7),
+            (4, 0, 6, 7, -1, 4, 4, 4, 4, 8, 8, 7, 8, 12, 12, 11),
+            (8, 0, 0, 2, 0, 1, 10, 11, -1, 8, 8, 8, 8, 12, 12, 11),
+            (12, 0, 0, 0, 8, 4, 14, 4, 12, 13, 8, 15, -1, 12, 12, 12),
+        ),
+    ),
+    (
+        (
+            (0, 4, 12, 7, 8, 1, 3, 6, 14, 13, 9, 11, 0, 5, 2, 10),
+            (1, 3, 5, 11, 0, 13, 12, 7, 6, 14, 10, 8, 9, 0, 4, 2),
+            (13, 9, 5, 8, 4, 2, 7, 11, 0, 12, 6, 10, 3, 1, 14, 0),
+            (7, 5, 12, 0, 6, 11, 1, 10, 9, 2, 14, 13, 0, 4, 8, 3),
+        ),
+        (
+            (0, 2, 8, 9, 13, 11, 3, 1, 14, 12, 7, 10, 4, 5, 0, 6),
+            (0, 2, 6, 11, 0, 13, 5, 8, 7, 14, 10, 12, 4, 9, 3, 1),
+            (11, 2, 6, 14, 4, 3, 9, 13, 0, 12, 7, 5, 10, 1, 8, 0),
+            (4, 6, 11, 5, 7, 10, 3, 9, 1, 12, 8, 14, 0, 0, 2, 13),
+        ),
+    ),
+)
+WAITS = (
+    (9, 3, 2, 8, 17, 16, 25, 6, 7, 5, 4, 24, 11, 10, 19, 21, 18, 15, 14, 20, 13, 12, 31, 30, 27, 26, 29, 28, 22, 23),
+    (0, 13, 1, 10, 11, 12, 15, 14, 24, 25, 6, 2, 3, 4, 17, 5, 16, 7, 29, 28, 23, 22, 30, 31, 26, 27, 21, 20, 19, 18),
+    (25, 9, 21, 8, 19, 18, 20, 23, 1, 22, 24, 0, 11, 10, 15, 13, 12, 27, 26, 14, 29, 28, 3, 2, 30, 31, 5, 4, 7, 6),
+    (16, 27, 17, 29, 26, 30, 28, 0, 31, 1, 9, 18, 19, 8, 20, 21, 2, 3, 4, 5, 23, 22, 11, 13, 10, 12, 14, 15, 6, 7),
+)
 
 
 def project(att, weight, tok):
@@ -323,8 +360,278 @@
     swap.wait_send()
 
 
+def shared(rows):
+    return all(row == rows[0] for row in rows)
+
+
+def quad_kernel(
+    plan, q_ref, k_ref, v_ref, order_hbm, w_ref, own_ref, att, w_buf, lse_ref,
+    order_ref, q_buf, kv, qt, acc, top, total,
+    kv_sem, q_sem, order_sem, send_sem, recv_sem, ready,
+    w_sem, a_sem,
+):
+    tok, width = q_ref.shape
+    group = width // DH
+    rows = group * tok
+    half = own_ref.shape[1]
+    head = lax.axis_index("head")
+    b = lax.axis_index("blk")
+    r = lax.axis_index("rep")
+    other = 1 - head
+    in_last = b // 3
+    in_third = b // 2 - in_last
+    in_second = b % 2 - in_last
+    step_x = 1 - 2 * (r % 2)
+    step_y = 2 - 4 * (r // 2)
+    depth = b + r % 2 + r // 2
+    mine_key = depth * 16 + b * 4 + r
+
+    def pick(values):
+        first, second, third, last = values
+        if shared(values):
+            return first
+        return first + in_second * (second - first) + in_third * (third - first) + in_last * (last - first)
+
+    def rep_at(rel):
+        return r + (rel % 2) * step_x + (rel // 2) * step_y
+
+    def key_of(code):
+        place, rep = code // 4, rep_at(code % 4)
+        return (place + rep % 2 + rep // 2) * 16 + place * 4 + rep
+
+    def device(code):
+        return {"blk": code // 4, "rep": rep_at(code % 4)}
+
+    def padded(lists):
+        longest = max(len(row) for row in lists)
+        return [
+            ([len(row) > i for row in lists], [row[i] if len(row) > i else row[0] if row else 0 for row in lists])
+            for i in range(longest)
+        ]
+
+    def each(lists, act):
+        for valid, codes in padded(lists):
+            code = pick(codes)
+            if all(valid):
+                act(code)
+            else:
+                pl.when(pick([int(ok) for ok in valid]) == 1)(functools.partial(act, code))
+
+    own = b * 4
+    loads = [
+        pltpu.make_async_copy(k_ref, kv.at[2 * own], kv_sem),
+        pltpu.make_async_copy(v_ref, kv.at[2 * own + 1], kv_sem),
+        pltpu.make_async_copy(q_ref, q_buf, q_sem),
+        pltpu.make_async_copy(order_hbm, order_ref, order_sem),
+    ]
+    for load in loads:
+        load.start()
+    barrier = pltpu.get_barrier_semaphore()
+
+    def greet(code):
+        @pl.when(key_of(code) > mine_key)
+        def _():
+            pl.semaphore_signal(barrier, inc=1, device_id=device(code), device_id_type=MESH)
+
+    each(plan["partners"], greet)
+
+    pl.semaphore_signal(barrier, inc=1, device_id={"head": other}, device_id_type=MESH)
+
+    earlier = 1
+    for valid, codes in padded(plan["partners"]):
+        code = pick(codes)
+        below = (mine_key + 4096 - key_of(code)) // 4096
+        earlier = earlier + below * (1 if all(valid) else pick([int(ok) for ok in valid]))
+    pl.semaphore_wait(barrier, earlier)
+
+    def announce(code):
+        @pl.when(key_of(code) < mine_key)
+        def _():
+            pl.semaphore_signal(
+                ready.at[b * 4 + code % 4], inc=1, device_id=device(code), device_id_type=MESH
+            )
+
+    each(plan["sources"], announce)
+
+    def send(slot, c, code, target, bucket):
+        return pltpu.make_async_remote_copy(
+            src_ref=kv.at[2 * slot + c], dst_ref=kv.at[2 * target + c],
+            send_sem=send_sem.at[bucket], recv_sem=recv_sem.at[2 * target + c],
+            device_id=device(code), device_id_type=MESH,
+        )
+
+    pltpu.make_async_copy(kv.at[pl.ds(2 * own, 2)], kv.at[pl.ds(2 * own, 2)], kv_sem).wait()
+
+    def spread(code, c):
+        send(own, c, code, own + code % 4, 0).start()
+
+    def spread_lower(entry):
+        code = entry // 2
+        @pl.when(key_of(code) < mine_key)
+        def _():
+            spread(code, entry % 2)
+
+    each(plan["own"], spread_lower)
+
+    loads[2].wait()
+    loads[3].wait()
+    for g in range(group):
+        qt[:, g * tok:(g + 1) * tok] = (
+            q_buf[:, g * DH:(g + 1) * DH].astype(jnp.float32).T.astype(jnp.bfloat16)
+        )
+    key_at = lax.broadcasted_iota(jnp.int32, (tok, rows), 0)
+    query_at = lax.broadcasted_iota(jnp.int32, (tok, rows), 1) % tok
+    lead = key_at - query_at
+    mine = order_ref[b * 4 + r]
+    factor = DH ** (-0.5) * math.log2(math.e)
+
+    def attend(slot, first=False):
+        scores = jnp.dot(kv[2 * slot], qt[...], preferred_element_type=jnp.float32) * factor
+        gap = (mine - order_ref[slot // 4 * 4 + rep_at(slot % 4)]) * tok
+        scores = jnp.where(lead <= gap, scores, NEG_FILL)
+        best = jnp.max(scores, axis=0, keepdims=True)
+        if not first:
+            before = top[...]
+            best = jnp.maximum(best, before)
+        weights = jnp.exp2(scores - best)
+        part = jnp.sum(weights, axis=0, keepdims=True)
+        numer = lax.dot_general(
+            kv[2 * slot + 1], weights.astype(jnp.bfloat16), (((0,), (0,)), ((), ())),
+            preferred_element_type=jnp.float32,
+        )
+        if first:
+            total[...] = part
+            acc[...] = numer
+        else:
+            shrink = jnp.exp2(before - best)
+            total[...] = total[...] * shrink + part
+            acc[...] = acc[...] * shrink + numer
+        top[...] = best
+
+    attend(own, True)
+
+    def await_ready(code):
+        @pl.when(key_of(code) > mine_key)
+        def _():
+            pl.semaphore_wait(ready.at[code], 1)
+
+    def spread_upper(entry):
+        code = entry // 4
+        @pl.when(key_of(code) > mine_key)
+        def _():
+            @pl.when(entry // 2 % 2 == 1)
+            def _():
+                pl.semaphore_wait(ready.at[code], 1)
+            spread(code, entry % 2)
+
+    each(plan["own_upper"], spread_upper)
+    each(plan["other_ready"], await_ready)
+
+    def remote(src, dst, sems):
+        return pltpu.make_async_remote_copy(
+            src_ref=src, dst_ref=dst, send_sem=sems.at[0], recv_sem=sems.at[1],
+            device_id={"head": other}, device_id_type=MESH,
+        )
+
+    w_local = pltpu.make_async_copy(
+        w_ref.at[:, pl.ds(pl.multiple_of(head * half, DH), half)], w_buf.at[0], w_sem.at[2]
+    )
+    w_remote = remote(w_ref.at[:, pl.ds(pl.multiple_of(other * half, DH), half)], w_buf.at[1], w_sem)
+    w_local.start()
+    w_remote.start()
+
+    done = 0
+    for at, (slots, halves, children) in enumerate(plan["steps"]):
+        slot, c = pick(slots), pick(halves)
+        send(slot, c, 0 * b, slot, 0).wait_recv()
+
+        def forward(entry):
+            code = entry // 16
+            send(slot, c, code, entry % 16, 1).start()
+
+        each(children, forward)
+        while done < len(plan["blocks"]) and plan["blocks"][done][0] <= at:
+            attend(pick(plan["blocks"][done][1]))
+            done += 1
+
+    att[0] = (acc[...] / total[...]).astype(jnp.bfloat16)
+    swap = remote(att.at[0], att.at[1], a_sem)
+    swap.start()
+    sums = (top[...] + jnp.log2(total[...])) * math.log(2.0)
+    for g in range(group):
+        lse_ref[g:g + 1, :] = sums[:, g * tok:(g + 1) * tok]
+
+    w_local.wait()
+    own_ref[...] = project(att[0], w_buf[0], tok)
+    for place in range(4):
+        @pl.when(b == place)
+        def _():
+            for bucket in (0, 1):
+                count = plan["sent"][bucket][place]
+                if count:
+                    sent = kv.at[pl.ds(0, count)]
+                    pltpu.make_async_copy(sent, sent, send_sem.at[bucket]).wait()
+    w_remote.wait()
+    swap.wait()
+
+
+def make_plan():
+    parents, ranks = TREES
+    own, sources, sinks = [[] for _ in range(4)], [set() for _ in range(4)], [set() for _ in range(4)]
+    forwards = {}
+    for c in (0, 1):
+        for z in range(4):
+            for t in sorted((t for t in range(16) if t != z * 4), key=lambda t: ranks[c][z][t]):
+                m = parents[c][z][t]
+                place, rel = m // 4, m % 4
+                code = t // 4 * 4 + (t % 4 ^ rel)
+                sinks[place].add(code)
+                sources[t // 4].add(place * 4 + (t % 4 ^ rel))
+                if m == z * 4:
+                    own[place].append((ranks[c][z][t], code, c))
+                else:
+                    forwards.setdefault((place, z * 4 + rel, c), []).append(code * 16 + z * 4 + t % 4)
+    own = [[(code, c) for _, code, c in sorted(row)] for row in own]
+    upper = []
+    for p, row in enumerate(own):
+        met, entries = set(), []
+        for code, c in sorted(row, key=lambda e: abs(e[0] // 4 - p) + e[0] % 2 + e[0] // 2 % 2):
+            entries.append(code * 4 + 2 * (code not in met) + c)
+            met.add(code)
+        upper.append(entries)
+    steps, blocks = [], []
+    for at in range(30):
+        waits = [WAITS[p][at] for p in range(4)]
+        steps.append((
+            [w // 2 for w in waits], [w % 2 for w in waits],
+            [forwards.get((p, waits[p] // 2, waits[p] % 2), []) for p in range(4)],
+        ))
+    complete = []
+    for p in range(4):
+        seen, row = set(), []
+        for at, w in enumerate(WAITS[p]):
+            if w // 2 in seen:
+                row.append((at, w // 2))
+            seen.add(w // 2)
+        complete.append(row)
+    for k in range(15):
+        blocks.append((max(complete[p][k][0] for p in range(4)), [complete[p][k][1] for p in range(4)]))
+    forwarded = [sum(len(v) for (place, _, _), v in forwards.items() if place == p) for p in range(4)]
+    return {
+        "partners": [sorted(sources[p] | sinks[p]) for p in range(4)],
+        "sources": [sorted(sources[p]) for p in range(4)],
+        "own": [[code * 2 + c for code, c in row] for row in own],
+        "own_upper": upper,
+        "other_ready": [sorted(sinks[p] - {code for code, _ in own[p]}) for p in range(4)],
+        "steps": steps,
+        "blocks": blocks,
+        "sent": [[len(row) for row in own], forwarded],
+    }
+
+
 def solution(mesh):
     spans = mesh.shape["blk"]
+    planned = spans == 4 and mesh.shape["rep"] == 4
 
     def body(queries, keys, values, stretch_order, out_weight):
         tok, width = queries.shape
@@ -334,8 +641,24 @@
         anywhere = pl.BlockSpec(memory_space=pltpu.HBM)
         vmem = pl.BlockSpec(memory_space=pltpu.VMEM)
         dma = pltpu.SemaphoreType.DMA
+        regular = pltpu.SemaphoreType.REGULAR
+        if planned:
+            run = functools.partial(quad_kernel, make_plan())
+            blocks = pltpu.VMEM((2 * 4 * spans, tok, DH), jnp.bfloat16)
+            sems = [dma, dma, dma, dma((2,)), dma((32,)), regular((16,)), dma((3,)), dma((2,))]
+        else:
+            run = functools.partial(kernel, spans)
+            blocks = pltpu.VMEM((4, spans, 2, tok, DH), jnp.bfloat16)
+            sems = [
+                dma((5,)), dma((4, 2)),
+                dma((spans, 4)), dma((spans, 2)),
+                dma((spans, 2)), dma((spans, 2)),
+                dma((spans, 2)), dma((spans, 2)),
+                dma((spans, 2)), dma((spans, 2)),
+                dma, dma, dma, dma,
+            ]
         gathered = pl.pallas_call(
-            functools.partial(kernel, spans),
+            run,
             out_shape=(
                 pltpu.VMEM((tok, half), jnp.float32),
                 pltpu.VMEM((2, DH, rows), jnp.bfloat16),
@@ -347,17 +670,12 @@
             scratch_shapes=[
                 pltpu.SMEM(stretch_order.shape, jnp.int32),
                 pltpu.VMEM((tok, width), jnp.bfloat16),
-                pltpu.VMEM((4, spans, 2, tok, DH), jnp.bfloat16),
+                blocks,
                 pltpu.VMEM((DH, rows), jnp.bfloat16),
                 pltpu.VMEM((DH, rows), jnp.float32),
                 pltpu.VMEM((1, rows), jnp.float32),
                 pltpu.VMEM((1, rows), jnp.float32),
-                dma((5,)), dma((4, 2)),
-                dma((spans, 4)), dma((spans, 2)),
-                dma((spans, 2)), dma((spans, 2)),
-                dma((spans, 2)), dma((spans, 2)),
-                dma((spans, 2)), dma((spans, 2)),
-                dma, dma, dma, dma,
+                *sems,
             ],
             compiler_params=pltpu.CompilerParams(collective_id=0, has_side_effects=True, vmem_limit_bytes=VMEM_LIMIT),
         )(*(

time: 22 us -> 20.4 us (0.927)
  the two profiles are of different devices: /device:TPU:0 before, /device:TPU:29 now
where the time goes in v1:
time: 20.4 us; the launch traced here: 20.2 us
  Pallas kernels  19.5 us (96%)
  between operations  0.64 us (3%)
    pallas_call x1, Pallas kernels, body(): pl.pallas_call(run, out_shape=(pltpu.VMEM((tok, half), jnp.float32), pltp...  18.3 us
    pallas_call x1, Pallas kernels, body(): pl.pallas_call(finish_kernel, out_shape=(jax.ShapeDtypeStruct((tok, half)...  1.24 us

profile of v1, /device:TPU:29, one launch (start us, length us, event | category | flops | bytes accessed | tf_op | source)
XLA Modules:
  0.0 20.2 jit_solution(15060007501508849067)
XLA Ops:
  0.6 18.3 %shard_map.68 = (f32[128,1536]{1,0:T(8,128)S(1)}, bf16[2,128,384]{2,1,0:T(8,128)(2,1)S(1)}, bf16[2,384,1536]{2,1,0:T(8,128)(2,1)S(1)}, f32[3,128]{1,0:T(4,128)S(1)}) custom-call(bf16[128,384]{1,0:T(8,128)(2,1)} %q_ref.1, bf16[128,128]{1,0:T(8,128)(2,1)} %k_ref.1, bf16[128,128]{1,0:T(8,128)(2,1)} %v_ref.1, s32[16]{0:T(128)} %order_hbm.1, bf16[384,3072]{1,0:T(8,128)(2,1)} %w_ref.1), custom_call_target="tpu_custom_call" | custom-call | tf_op jit(solution)/shard_map/pallas_call | solution.py:660
  18.9 1.2 %shard_map.69 = (bf16[128,1536]{1,0:T(8,128)(2,1)}, f32[3,128]{1,0:T(4,128)}) custom-call(f32[128,1536]{1,0:T(8,128)S(1)} %get-tuple-element.6.own_ref, bf16[2,128,384]{2,1,0:T(8,128)(2,1)S(1)} %get-tuple-element.7.att, bf16[2,384,1536]{2,1,0:T(8,128)(2,1)S(1)} %get-tuple-element.8.w_buf, f32[3,128]{1,0:T(4,128)S(1)} %get-tuple-element.9.sums_ref), custom_call_target="tpu_custom_call" | custom-call | tf_op jit(solution)/shard_map/pallas_call | solution.py:685
